TPU v7x, 32 devices: a whole 2x2x4 slice. The times are simulated.
32 devices in a mesh: sta: 8 (over z, core), cell: 4 (over y, x).
Axes of the slice: x: 2, y: 2, z: 4, core: 2. Of those that a mesh axis runs over, the one named last changes fastest.
Arguments:
- station_xyz: float32 [3, 2048], P(None, 'sta'), may hold values from 0 to 1, as said below
- cell_xyz: float32 [3, 131072], P(None, 'cell'), may hold values from -0.6 to 1, as said below
- cell_weight: float32 [131072], P('cell'), may hold values from 0.3 to 3
- data: float32 [2048], P(('sta', 'cell')), may hold values from -6 to 6
- model_start: float32 [131072], P(('cell', 'sta')), may hold values from -6 to 6
Outputs:
- model_next: float32 [131072], P(('cell', 'sta'))
- residual_next: float32 [2048], P(('sta', 'cell'))
- search_next: float32 [131072], P(('cell', 'sta'))
Inputs may be any that keep to these rules, and one draw needn't show every extreme that they name: `station_xyz`: rows 0 and 1 lie in [0, 1), row 2 in [0, 0.05]. `cell_xyz`: rows 0 and 1 lie in [0, 1), row 2 in [-0.6, -0.02].
All inputs are finite; a program needn't handle non-finite values.
Results may differ from a plain program's by a relative error of at most 0.0003.
Values sent between devices are 32-bit elements; how exact they have to be, the bound alone decides.
A program may use at most 64 MiB of HBM per device.

v0:
```python
import functools
import math

import jax
import jax.numpy as jnp
from jax import lax
from jax.experimental import pallas as pl
from jax.experimental.pallas import tpu as pltpu
from jax.sharding import PartitionSpec as P

SOFT = 0.0001
LANES = 128
FEATURES = 96
MESH = pl.DeviceIdType.MESH
F32 = jnp.float32


def bf_pieces(x):
    a = x.astype(jnp.bfloat16).astype(F32)
    b = (x - a).astype(jnp.bfloat16).astype(F32)
    c = (x - a - b).astype(jnp.bfloat16).astype(F32)
    return a, b, c


def coordinate_pieces(x):
    row = lax.broadcasted_iota(jnp.int32, x.shape, 0)
    shift = jnp.where(row < 2, -0.5, jnp.where(row == 2, 0.275, 0.0))
    x = jnp.where(row < 3, x + shift, 0.0)
    h = jnp.round(x * 256.0) * (1.0 / 256.0)
    rest = x - h
    m = jnp.round(rest * 65536.0) * (1.0 / 65536.0)
    l = (rest - m).astype(jnp.bfloat16).astype(F32)
    return row, h, m, l


def norm_pieces(h, m, l, soft):
    a = jnp.sum(h * h, axis=0, keepdims=True)
    ml = m + l
    b = jnp.sum(2.0 * h * ml + ml * ml, axis=0, keepdims=True) + soft
    a1 = jnp.round(a * 256.0) * (1.0 / 256.0)
    return (a1, a - a1) + bf_pieces(b)


def rows_of(row, items):
    out = jnp.zeros(row.shape, F32)
    for at, item in items.items():
        out = jnp.where(row == at, item, out)
    return out


def cell_features(x, u, w):
    row, h, m, l = coordinate_pieces(x)
    a1, a2, b1, b2, b3 = norm_pieces(h, m, l, 0.0)
    first = h + rows_of(row, {3: 1.0, 4: 1.0, 5: a1, 6: a2})
    norms = rows_of(row, {0: 1.0, 1: 1.0, 2: 1.0, 3: b1, 4: b2, 5: b3})
    u1, u2, u3 = bf_pieces(u)
    w1, w2, w3 = bf_pieces(w)
    vectors = rows_of(row, {0: u1, 1: u2, 2: u3, 3: w1, 4: w2, 5: w3})
    zero = jnp.zeros_like(x)
    return jnp.concatenate([first, h, h, m, m, m, l, l, l, norms, vectors, zero], axis=0)


def station_features(x):
    row, h, m, l = coordinate_pieces(x)
    a1, a2, b1, b2, b3 = norm_pieces(h, m, l, SOFT)
    first = -2.0 * h + rows_of(row, {3: a1, 4: a2, 5: 1.0, 6: 1.0})
    norms = rows_of(row, {0: b1, 1: b2, 2: b3, 3: 1.0, 4: 1.0, 5: 1.0})
    h, m, l = -2.0 * h, -2.0 * m, -2.0 * l
    zero = jnp.zeros_like(x)
    return jnp.concatenate([first, m, l, h, m, l, h, m, l, norms, zero, zero], axis=0)


def spread_matrix():
    row = lax.broadcasted_iota(jnp.int32, (FEATURES, 3 * LANES), 0)
    col = lax.broadcasted_iota(jnp.int32, (FEATURES, 3 * LANES), 1)
    z = (row == 2) | (row == 26) | (row == 50)
    u = (row >= 80) & (row < 83)
    w = (row >= 83) & (row < 86)
    pick = ((col < LANES) & z) | ((col >= LANES) & (col < 2 * LANES) & u) | ((col >= 2 * LANES) & w)
    return jnp.where(pick, 1.0, 0.0).astype(jnp.bfloat16)


def kernel(sizes, st_ref, cell_ref, w_ref, m_ref, data_ref, model_ref, res_ref, search_ref,
           kmat, lhs, czb, ub, wb, gb, grow, st_all, szb, rbc, rs1, rs2, ag1, ag2, gm, gn, out1, out2,
           send_sem, recv_sem):
    n_sta, n_cell, cells, width, piece, scale, mb = sizes
    n = n_sta * n_cell
    groups = cells // 8
    blocks = cells // LANES
    per_tile = LANES // piece
    tiles = width // LANES
    my_sta, my_cell = lax.axis_index("sta"), lax.axis_index("cell")
    me = my_sta * n_cell + my_cell

    def peer(k):
        flat = lax.rem(me + k, n)
        return (flat // n_cell, lax.rem(flat, n_cell))

    barrier = pltpu.get_barrier_semaphore()

    def greet(k, c):
        pl.semaphore_signal(barrier, inc=1, device_id=peer(k), device_id_type=MESH)
        return c

    lax.fori_loop(1, n, greet, 0)

    lane = lax.broadcasted_iota(jnp.int32, (1, LANES), 1)
    own = lane < piece

    spread = spread_matrix()

    def prepare(b, c):
        at = pl.multiple_of(b * LANES, LANES)
        cols = pl.ds(at, LANES)
        w = w_ref[:, cols] * scale
        feats = cell_features(cell_ref[:, cols], w * m_ref[:, cols], w)
        rows = jnp.transpose(feats).astype(jnp.bfloat16)
        lhs[cols, :] = rows
        wide = jnp.dot(rows, spread, preferred_element_type=F32)
        gs = pl.ds(b * (LANES // 8), LANES // 8)
        czb[gs] = wide[:, :LANES].reshape(LANES // 8, 8, LANES) - 0.275
        ub[gs] = wide[:, LANES:2 * LANES].reshape(LANES // 8, 8, LANES)
        wb[gs] = wide[:, 2 * LANES:].reshape(LANES // 8, 8, LANES)
        return c

    lax.fori_loop(0, blocks, prepare, 0, unroll=4)

    st_all[my_sta] = st_ref[...]
    pl.semaphore_wait(barrier, n - 1)

    def send_stations(k, c):
        pltpu.make_async_remote_copy(
            src_ref=st_ref, dst_ref=st_all.at[my_sta], send_sem=send_sem.at[0], recv_sem=recv_sem.at[0],
            device_id=(lax.rem(my_sta + k, n_sta), my_cell), device_id_type=MESH).start()
        return c

    lax.fori_loop(1, n_sta, send_stations, 0)

    def bulk_wait(buf, count, sems, which):
        part = buf.at[pl.ds(0, count)]
        pltpu.make_async_copy(part, part, sems.at[which]).wait()

    def send_block(out, rs, which, s, rows):
        row = jnp.concatenate(rows, axis=1)
        out[s] = row
        rs[me, s] = row

        def one(k, c):
            pltpu.make_async_remote_copy(
                src_ref=out.at[s], dst_ref=rs.at[me, s], send_sem=send_sem.at[which],
                recv_sem=recv_sem.at[which], device_id=peer(k), device_id_type=MESH).start()
            return c

        lax.fori_loop(1, n, one, 0)

    def own_piece(row):
        out = jnp.zeros((1, LANES), F32)
        for c in range(n_cell):
            tile, q = (c * piece) // LANES, c % per_tile
            value = row[:, tile * LANES:(tile + 1) * LANES]
            if q:
                value = pltpu.roll(value, LANES - q * piece, 1)
            out = jnp.where(my_cell == c, value, out)
        return out

    def broadcast(buf, which):
        def one(k, c):
            pltpu.make_async_remote_copy(
                src_ref=buf.at[me], dst_ref=buf.at[me], send_sem=send_sem.at[which],
                recv_sem=recv_sem.at[which], device_id=peer(k), device_id_type=MESH).start()
            return c
        lax.fori_loop(1, n, one, 0)

    def total(buf):
        return jnp.sum(buf[...], axis=0)

    def sta_block(k, c):
        s = lax.rem(my_sta + k, n_sta)

        @pl.when(k == 1)
        def _():
            bulk_wait(st_all, n_sta - 1, recv_sem, 0)

        x = st_all[s]
        rhs = station_features(x).astype(jnp.bfloat16)
        sz = jnp.broadcast_to(x[2:3, :], (8, width))

        def block(b, accs):
            at = pl.multiple_of(b * mb, mb)
            r2 = jnp.dot(lhs[pl.ds(at, mb), :], rhs, preferred_element_type=F32)
            gs = pl.ds(b * (mb // 8), mb // 8)
            cz, u = czb[gs], ub[gs]
            out = []
            for t in range(tiles):
                part = r2[:, t * LANES:(t + 1) * LANES].reshape(mb // 8, 8, LANES)
                inv = lax.rsqrt(part)
                dz = sz[None, :, t * LANES:(t + 1) * LANES] - cz
                value = (dz * inv) * (inv * inv)
                kmat[s, gs, :, t * LANES:(t + 1) * LANES] = value
                out.append(accs[t] + jnp.sum(value * u, axis=0))
            return tuple(out)

        accs = lax.fori_loop(0, cells // mb, block, tuple(jnp.zeros((8, LANES), F32) for _ in range(tiles)))
        rows = [jnp.sum(a, axis=0, keepdims=True) for a in accs]
        first = jnp.where(k == 0, 1.0, 0.0)
        for q in range(n_cell):
            tile, at = (q * piece) // LANES, q % per_tile
            value = jnp.where(own, data_ref[...], 0.0) * jnp.where(my_cell == q, first, 0.0)
            if at:
                value = pltpu.roll(value, at * piece, 1)
            rows[tile] = rows[tile] - value
        send_block(out1, rs1, 1, s, rows)
        return c

    lax.fori_loop(0, n_sta, sta_block, 0)
    bulk_wait(rs1, n - 1, recv_sem, 1)

    def residual(s, c):
        row = -jnp.sum(rs1[:, s], axis=0)
        ag1[s] = row
        rbc[s] = jnp.broadcast_to(row, (8, width))
        return c

    lax.fori_loop(0, n_sta, residual, 0)

    step = 8

    def backward(b, c):
        gs = pl.ds(b * step, step)
        acc = jnp.zeros((step, 8, LANES), F32)
        for s in range(n_sta):
            for t in range(tiles):
                cols = slice(t * LANES, (t + 1) * LANES)
                acc = acc + kmat[s, gs, :, cols] * rbc[s, :, cols][None]
        gb[gs] = acc
        return c

    ones = jnp.ones((3 * LANES, LANES), jnp.bfloat16)
    eye = (lax.broadcasted_iota(jnp.int32, (16, 8, LANES), 0) * 8
           + lax.broadcasted_iota(jnp.int32, (16, 8, LANES), 1)
           == lax.broadcasted_iota(jnp.int32, (16, 8, LANES), 2))

    def finish(dst, b, sq):
        gs = pl.ds(b * 16, 16)
        parts = jnp.concatenate(bf_pieces(gb[gs].reshape(LANES, LANES)), axis=1).astype(jnp.bfloat16)
        w = wb[gs]
        g = jnp.dot(parts, ones, preferred_element_type=F32).reshape(16, 8, LANES) * w
        ub[gs] = g * w
        row = jnp.sum(jnp.sum(jnp.where(eye, g, 0.0), axis=0), axis=0, keepdims=True)
        dst[:, pl.ds(pl.multiple_of(b * LANES, LANES), LANES)] = row
        return sq + row * row

    def gradient(dst):
        lax.fori_loop(0, groups // step, backward, 0)
        sq = lax.fori_loop(0, blocks, functools.partial(finish, dst), jnp.zeros((1, LANES), F32), unroll=4)
        return jnp.broadcast_to(jnp.sum(sq, axis=1, keepdims=True), (1, LANES))

    gm[me] = gradient(grow)
    broadcast(gm, 2)

    together = 4

    def image_block(k, c):
        ss = [lax.rem(my_sta + k * together + i, n_sta) for i in range(together)]

        def block(b, accs):
            gs = pl.ds(b * 8, 8)
            u = ub[gs]
            out = []
            for i in range(together):
                for t in range(tiles):
                    value = kmat[ss[i], gs, :, t * LANES:(t + 1) * LANES] * u
                    out.append(accs[i * tiles + t] + jnp.sum(value, axis=0))
            return tuple(out)

        accs = lax.fori_loop(0, groups // 8, block,
                             tuple(jnp.zeros((8, LANES), F32) for _ in range(together * tiles)))
        for i in range(together):
            rows = [jnp.sum(a, axis=0, keepdims=True) for a in accs[i * tiles:(i + 1) * tiles]]
            send_block(out2, rs2, 3, ss[i], rows)
        return c

    lax.fori_loop(0, n_sta // together, image_block, 0)
    bulk_wait(gm, n - 1, recv_sem, 2)
    gamma = total(gm)[:, :1]
    bulk_wait(rs2, n - 1, recv_sem, 3)

    def image_sum(s, sq):
        row = jnp.sum(rs2[:, s], axis=0)
        ag2[s] = row
        return sq + row * row

    sq = lax.fori_loop(0, n_sta, image_sum, jnp.zeros((1, width), F32))
    alpha = gamma / jnp.sum(sq, axis=1, keepdims=True)

    def residual_next(s, c):
        rbc[s] = jnp.broadcast_to(ag1[s] - alpha * ag2[s], (8, width))
        return c

    lax.fori_loop(0, n_sta, residual_next, 0)
    res_ref[...] = own_piece(ag1[my_sta] - alpha * ag2[my_sta])

    gn[me] = gradient(search_ref)
    broadcast(gn, 5)
    model_ref[...] = m_ref[...] + alpha * grow[...]
    bulk_wait(gn, n - 1, recv_sem, 5)
    beta = total(gn)[:, :1] / gamma
    search_ref[...] = search_ref[...] + beta * grow[...]

    bulk_wait(st_all, n_sta - 1, send_sem, 0)
    for which, buf in ((1, rs1), (2, gm), (3, rs2), (5, gn)):
        bulk_wait(buf, n - 1, send_sem, which)


def per_device(station_xyz, cell_xyz, cell_weight, data, model_start):
    n_sta, n_cell = lax.axis_size("sta"), lax.axis_size("cell")
    n = n_sta * n_cell
    width = station_xyz.shape[1]
    cells = model_start.shape[0]
    piece = data.shape[0]
    scale = 1.0 / math.sqrt(width * n_sta * cells * n)
    at = lax.axis_index("sta") * cells
    own_cells = jnp.pad(lax.dynamic_slice_in_dim(cell_xyz, at, cells, 1), ((0, 5), (0, 0)))
    own_weight = lax.dynamic_slice_in_dim(cell_weight, at, cells, 0).reshape(1, cells)
    stations = jnp.pad(station_xyz, ((0, 5), (0, 0)))
    data_row = jnp.pad(data, (0, LANES - piece)).reshape(1, LANES)
    groups = cells // 8
    mb = min(2048, cells)
    sizes = (n_sta, n_cell, cells, width, piece, scale, mb)
    vmem = pl.BlockSpec(memory_space=pltpu.VMEM)
    wide = pltpu.VMEM((groups, 8, LANES), F32)
    whole = pltpu.VMEM((n, n_sta, 1, width), F32)
    line = pltpu.VMEM((n_sta, 1, width), F32)
    message = pltpu.VMEM((n, 1, LANES), F32)
    model_next, residual, search = pl.pallas_call(
        functools.partial(kernel, sizes),
        out_shape=(jax.ShapeDtypeStruct((1, cells), F32), jax.ShapeDtypeStruct((1, LANES), F32),
                   jax.ShapeDtypeStruct((1, cells), F32)),
        in_specs=[vmem] * 5,
        out_specs=(vmem, vmem, vmem),
        scratch_shapes=[
            pltpu.VMEM((n_sta, groups, 8, width), F32),
            pltpu.VMEM((cells, FEATURES), jnp.bfloat16),
            wide, wide, wide, wide,
            pltpu.VMEM((1, cells), F32),
            pltpu.VMEM((n_sta, 8, width), F32),
            pltpu.VMEM((n_sta, 8, width), F32),
            pltpu.VMEM((n_sta, 8, width), F32),
            whole, whole, line, line, message, message, line, line,
            pltpu.SemaphoreType.DMA((6,)),
            pltpu.SemaphoreType.DMA((6,)),
        ],
        compiler_params=pltpu.CompilerParams(
            collective_id=0, has_side_effects=True, vmem_limit_bytes=60 * 1024 * 1024),
    )(stations, own_cells, own_weight, model_start.reshape(1, cells), data_row)
    return (model_next.reshape(cells), residual[0, :piece], search.reshape(cells))


def solution(mesh):
    placed = (P(None, "sta"), P(None, "cell"), P("cell"), P(("sta", "cell")), P(("cell", "sta")))
    return jax.shard_map(
        per_device,
        mesh=mesh,
        in_specs=placed,
        out_specs=(P(("cell", "sta")), P(("sta", "cell")), P(("cell", "sta"))),
        check_vma=False,
    )
```

profile of v0, /device:TPU:0, one launch (start us, length us, event | category | flops | bytes accessed | tf_op | source)
XLA Modules:
  0.0 66.9 jit_solution(383503618386003162)
XLA Ops:
  0.6 0.0 copy-start
  0.7 1.0 %copy-done = f32[3,32768]{1,0:T(4,128)S(1)} copy-done((f32[3,32768]{1,0:T(4,128)S(1)}, f32[3,32768]{1,0:T(4,128)}, u32[]{:S(2)}) %copy-start) | copy-done | bytes 393240
  1.7 0.7 pad.13.cell_ref
  2.4 0.0 copy-start.2
  2.4 1.3 %dynamic_slice.7 = f32[4096]{0:T(1024)} dynamic-slice(f32[32768]{0:T(1024)} %param.7, s32[]{:T(128)S(6)} %select_n.4), dynamic_slice_sizes={4096} | dynamic-slice | bytes 32772 | tf_op jit(solution)/shard_map/dynamic_slice | solution.py:324
  3.7 0.0 copy-done.2
  3.7 0.0 copy-start.3
  3.7 0.6 pad.12.st_ref
  4.3 0.1 copy-done.3
  4.4 0.5 pad_bitcast_fusion.data_ref
  4.9 58.9 %shard_map.76 = (f32[1,4096]{1,0:T(1,128)}, f32[1,128]{1,0:T(1,128)}, f32[1,4096]{1,0:T(1,128)}) custom-call(f32[8,256]{1,0:T(8,128)} %pad.12.st_ref, f32[8,4096]{1,0:T(8,128)} %pad.13.cell_ref, f32[1,4096]{1,0:T(1,128)} %bitcast.8, f32[1,4096]{1,0:T(1,128)} %bitcast.11, f32[1,128]{1,0:T(1,128)} %pad_bitcast_fusion.data_ref), custom_call_target="tpu_custom_call" | custom-call | tf_op jit(solution)/shard_map/pallas_call | solution.py:335
  63.7 0.0 copy-start.4
  63.8 0.7 copy-done.4
  64.4 0.5 slice_bitcast_fusion
  64.9 0.0 copy-start.1
  64.9 1.3 %copy.10 = f32[4096]{0:T(1024)} copy(f32[4096]{0:T(1024)} %bitcast.10) | data formatting | bytes 32768
  66.3 0.0 copy-done.1
  66.3 0.6 copy.11
  (1 shorter events, 0.0 us)
Async XLA Ops:
  0.6 1.0 %copy-start = (f32[3,32768]{1,0:T(4,128)S(1)}, f32[3,32768]{1,0:T(4,128)}, u32[]{:S(2)}) copy-start(f32[3,32768]{1,0:T(4,128)} %param.6) | copy-start | bytes 1179652
  2.4 1.3 %copy-start.2 = (f32[3,256]{1,0:T(4,128)S(1)}, f32[3,256]{1,0:T(4,128)}, u32[]{:S(2)}) copy-start(f32[3,256]{1,0:T(4,128)} %param.5) | copy-start | bytes 9220
  3.7 0.7 copy-start.3
  63.7 0.7 copy-start.4
  64.9 1.3 %copy-start.1 = (f32[1,4096]{1,0:T(1,128)S(1)}, f32[1,4096]{1,0:T(1,128)}, u32[]{:S(2)}) copy-start(f32[1,4096]{1,0:T(1,128)} %get-tuple-element.8) | copy-start | bytes 49156
where the time goes:
time: 67.2 us; the launch traced here: 66.9 us
  Pallas kernels  58.9 us (88%)
  local copies, waits for them, and re-layouts  7.33 us (11%)
    pallas_call x1, Pallas kernels, per_device(): pl.pallas_call(functools.partial(kernel, sizes), out_shape=(jax.ShapeDtyp...  58.9 us
    unnamed x12, local copies, waits for them, and re-layouts  3.7 us

commit v1 on v0

v1 whole, which is shorter than its diff:
```python
import functools
import math

import jax
import jax.numpy as jnp
import numpy as np
from jax import lax
from jax.experimental import pallas as pl
from jax.experimental.pallas import tpu as pltpu
from jax.sharding import PartitionSpec as P

SOFT = float(np.float32(0.0001))


def split(value):
    out = []
    for _ in range(3):
        scale = 2.0 ** (math.floor(math.log2(value)) - 7)
        out.append(math.floor(value / scale) * scale)
        value -= out[-1]
    return out


SOFT_PIECES = split(SOFT)
LANES = 128
FEATURES = 80
MESH = pl.DeviceIdType.MESH
F32 = jnp.float32
BF16 = jnp.bfloat16


def pieces(x):
    row = lax.broadcasted_iota(jnp.int32, x.shape, 0)
    x = x + jnp.where(row < 2, -0.5, 0.275)
    x = jnp.where(row < 3, x, 0.0)
    h = jnp.round(x * 256.0) * (1.0 / 256.0)
    rest = x - h
    m = jnp.round(rest * 65536.0) * (1.0 / 65536.0)
    l = rest - m
    a = h * h
    a1 = jnp.round(a * 256.0) * (1.0 / 256.0)
    b = 2.0 * h * rest + rest * rest
    b1 = jnp.round(b * 131072.0) * (1.0 / 131072.0)
    return row, h, m, l, (a1, a - a1, b1, b - b1)


def pair(first, second):
    return first + pltpu.roll(second, 3, 0)


def eight_rows(x):
    return jnp.concatenate([x, jnp.zeros((8 - x.shape[0], x.shape[1]), F32)], axis=0)


def cell_features(x):
    row, h, m, l, (a1, a2, b1, b2) = pieces(x)
    ones = jnp.ones_like(x)
    zero = jnp.zeros_like(x)
    return jnp.concatenate([pair(h, h), pair(h, m), pair(m, m), pair(l, l), l, pair(a1, a2),
                            pair(b1, b2), ones, ones, zero], axis=0).astype(BF16)


def station_features(x):
    row, h, m, l, (a1, a2, b1, b2) = pieces(x)
    ones = jnp.where(row < 6, 1.0, 0.0)
    soft = jnp.where(row == 6, SOFT_PIECES[0], 0.0) + jnp.where(row == 7, SOFT_PIECES[1], 0.0)
    rest = jnp.where(row == 6, SOFT_PIECES[2], 0.0)
    zero = jnp.zeros_like(x)
    h2, m2, l2 = -2.0 * h, -2.0 * m, -2.0 * l
    return jnp.concatenate([pair(h2, m2), pair(l2, h2), pair(m2, l2), pair(h2, m2), l2, ones,
                            ones, pair(a1, a2) + soft, pair(b1, b2) + rest, zero], axis=0)


def kernel(sizes, st_hbm, cell_hbm, w_hbm, m_hbm, data_ref, model_ref, res_ref, search_ref,
           kmat, rhs, lhs, cell_v, w_v, m_all, st_all, szb, urow, acc, gacc, rb, rrow, qrow, grow,
           out1, out2, rs1, rs2, part1, part2, gather1, gather2, gmsg, gnmsg, gout, gnout, dout, din, drow,
           in_sem, st_send, st_recv, m_sem, ar_send, ar_recv1, ar_recv2, ex_send, ex_recv1, ex_recv2,
           sc_send, sc_recv, r2a, r2b):
    n_sta, n_cell, cells, width, piece, scale = sizes
    nz = n_sta // 2
    chips = nz * n_cell
    tiles = 2 * cells // LANES
    half = cells // LANES
    groups = width // 8
    high = width // LANES
    per_tile = LANES // piece
    my_sta, my_cell = lax.axis_index("sta"), lax.axis_index("cell")
    core = lax.rem(my_sta, 2)
    z = lax.div(my_sta, 2)
    chip = z * n_cell + my_cell
    partner = (z * 2 + 1 - core, my_cell)

    def peer(k):
        flat = lax.rem(chip + k, chips)
        return (lax.div(flat, n_cell) * 2 + core, lax.rem(flat, n_cell))

    def every_peer(act):
        if chips > 16 or chips & (chips - 1) or n_cell & (n_cell - 1):
            def one(k, c):
                act(peer(k))
                return c

            lax.fori_loop(1, chips, one, 0)
        else:
            for k in range(1, chips):
                act((my_sta ^ (k // n_cell * 2), my_cell ^ (k % n_cell)))

    def remote(src, dst, send, recv, device):
        return pltpu.make_async_remote_copy(src_ref=src, dst_ref=dst, send_sem=send, recv_sem=recv,
                                            device_id=device, device_id_type=MESH)

    def drain(ref, sem):
        pltpu.make_async_copy(ref, ref, sem).wait()

    first_cell = pl.multiple_of(z * 2 * cells, 2 * cells)
    first_row = pl.multiple_of(z * tiles, tiles)
    load_cells = pltpu.make_async_copy(cell_hbm.at[:, pl.ds(first_cell, 2 * cells)], cell_v, in_sem.at[0])
    load_stations = pltpu.make_async_copy(st_hbm, st_all.at[z], in_sem.at[1])
    load_weights = pltpu.make_async_copy(w_hbm.at[pl.ds(first_row, tiles)], w_v, in_sem.at[2])
    load_model = pltpu.make_async_copy(m_hbm, m_all.at[core], in_sem.at[3])
    load_cells.start()
    load_stations.start()
    load_weights.start()
    load_model.start()

    barrier = pltpu.get_barrier_semaphore()

    every_peer(lambda device: pl.semaphore_signal(barrier, inc=1, device_id=device, device_id_type=MESH))
    pl.semaphore_signal(barrier, inc=1, device_id=partner, device_id_type=MESH)

    def features(n, c):
        cols = pl.ds(pl.multiple_of(n * 512, 512), 512)
        rhs[:, cols] = cell_features(eight_rows(cell_v[:, cols]))
        return c

    load_cells.wait()
    lax.fori_loop(0, 2 * cells // 512, features, 0)

    def prepare(b):
        x = eight_rows(st_all[b])
        feats = station_features(x)
        for i in range(high):
            cols = slice(i * LANES, (i + 1) * LANES)
            lhs[cols, :] = jnp.transpose(feats[:, cols]).astype(BF16)
            zz = jnp.transpose(jnp.broadcast_to(x[2:3, cols], (LANES, LANES)))
            szb[i * 16:(i + 1) * 16] = zz.reshape(16, 8, LANES)

    block = 512
    per_block = block // LANES

    def distances(n, r2):
        cols = pl.ds(pl.multiple_of(n * block, block), block)
        r2[...] = jnp.dot(lhs[...], rhs[:, cols], preferred_element_type=F32).reshape(groups, 8, block)

    def values(b, n, r2):
        at = n * block
        czs = []
        cols = []
        for t in range(per_block):
            cols.append(pl.ds(pl.multiple_of(at + t * LANES, LANES), LANES))
            czs.append(jnp.broadcast_to(cell_v[2:3, cols[t]], (8, LANES)))
        for g in range(groups):
            sz = szb[g]
            for t in range(per_block):
                inv = lax.rsqrt(r2[g, :, t * LANES:(t + 1) * LANES])
                kmat[b * groups + g, :, cols[t]] = ((sz - czs[t]) * inv) * (inv * inv)

    def build(b):
        count = 2 * cells // block
        distances(0, r2a)

        def one(i, c):
            distances(i * 2 + 1, r2b)
            values(b, i * 2, r2a)
            distances(lax.rem(i * 2 + 2, count), r2a)
            values(b, i * 2 + 1, r2b)
            return c

        lax.fori_loop(0, count // 2, one, 0)

    step = 4

    def forward(b, h, add):
        us = [jnp.broadcast_to(urow[pl.ds(h * half + t, 1), :], (8, LANES)) for t in range(half)]

        def some(i, c):
            for j in range(step):
                g = i * step + j
                sums = [None] * 4
                for t in range(half):
                    cols = pl.ds(pl.multiple_of(h * cells + t * LANES, LANES), LANES)
                    value = kmat[b * groups + g, :, cols] * us[t]
                    sums[t % 4] = value if sums[t % 4] is None else sums[t % 4] + value
                value = (sums[0] + sums[1]) + (sums[2] + sums[3])
                acc[b * groups + g] = value + acc[b * groups + g] if add else value
            return c

        lax.fori_loop(0, groups // step, some, 0)

    def block_rows(b):
        rows = []
        for i in range(high):
            x = acc[pl.ds(b * groups + i * 16, 16)].reshape(LANES, LANES)
            rows.append(jnp.sum(jnp.transpose(x), axis=0, keepdims=True))
        return jnp.concatenate(rows, axis=0)

    def send_rows(rows, out, rs, recv, b, which=0):
        out[b] = rows
        rs[b, chip] = rows

        every_peer(lambda device: remote(out.at[b], rs.at[b, chip], ar_send.at[which], recv.at[b],
                                         device).start())

    def broadcast(value, out, msgs, which):
        out[...] = value
        msgs[chip] = value

        every_peer(lambda device: remote(out, msgs.at[chip], sc_send.at[which], sc_recv.at[which],
                                         device).start())

    def order(k):
        return jnp.where(k <= z, z - k, k)

    def settled(j):
        mid = nz // 2
        return jnp.where(lax.rem(j, 2) == 0, mid - 1 - lax.div(j, 2), mid + lax.div(j, 2))

    load_stations.wait()
    prepare(z)
    build(z)

    pl.semaphore_wait(barrier, chips)

    def send_stations(k, c):
        other = lax.rem(z + k, nz)
        remote(st_all.at[z], st_all.at[z], st_send, st_recv.at[z], (other * 2 + core, my_cell)).start()
        return c

    lax.fori_loop(1, nz, send_stations, 0)
    load_model.wait()
    remote(m_all.at[core], m_all.at[core], m_sem.at[0], m_sem.at[1], partner).start()
    load_weights.wait()
    ws = w_v[...] * scale
    w_v[...] = ws
    drain(m_all.at[0], m_sem.at[1])
    urow[...] = ws * m_all[...].reshape(tiles, LANES)

    data = data_ref[...]
    drow[...] = jnp.zeros((high, LANES), F32)
    lane = lax.broadcasted_iota(jnp.int32, (1, LANES), 1)
    wide = jnp.where(lane < piece, jnp.concatenate([data] * per_tile, axis=1), 0.0)
    for q in range(n_cell):
        tile, at = q // per_tile, q % per_tile
        value = pltpu.roll(wide, at * piece, 1) if at else wide
        drow[tile:tile + 1, :] += jnp.where(my_cell == q, value, 0.0)

    forward(z, 0, False)
    forward(z, 1, True)
    send_rows(block_rows(z) - drow[...], out1, rs1, ar_recv1, z)

    def rest(k, c):
        b = order(k)
        drain(st_all.at[b], st_recv.at[b])
        prepare(b)
        build(b)
        forward(b, 0, False)
        forward(b, 1, True)
        send_rows(block_rows(b), out1, rs1, ar_recv1, b)
        return c

    lax.fori_loop(1, nz, rest, 0)

    def arrive(b, rs, recv, store, sign):
        drain(rs.at[b, pl.ds(0, chips - 1)], recv.at[b])
        row = sign * jnp.sum(rs[b], axis=0)
        store[b] = row
        for i in range(high):
            x = jnp.transpose(jnp.broadcast_to(row[i:i + 1], (LANES, LANES)))
            rb[i * 16:(i + 1) * 16] = x.reshape(16, 8, LANES)

    strip = 8

    def backward(b, at):
        rs_ = [rb[g] for g in range(groups)]
        cols = [pl.ds(pl.multiple_of((at + t) * LANES, LANES), LANES) for t in range(strip)]
        out = []
        for t in range(strip):
            total = gacc[at + t]
            for g in range(groups):
                total = total + kmat[b * groups + g, :, cols[t]] * rs_[g]
            out.append(total)
        return out

    def gradient(rs, recv, store, sign, part, gather, send, ex_recv, complete):
        gacc[...] = jnp.zeros((tiles, 8, LANES), F32)

        def early(j, c):
            b = settled(j)
            arrive(b, rs, recv, store, sign)

            def some(i, c):
                for t, total in enumerate(backward(b, i * strip)):
                    gacc[i * strip + t] = total
                return c

            lax.fori_loop(0, tiles // strip, some, 0)
            return c

        lax.fori_loop(0, nz - 1, early, 0)
        b = settled(nz - 1)
        arrive(b, rs, recv, store, sign)
        complete()
        for h in range(2):
            def some(i, c):
                rows = [jnp.sum(a, axis=0, keepdims=True) for a in backward(b, h * half + i * strip)]
                part[h, pl.ds(pl.multiple_of(i * strip, strip), strip)] = jnp.concatenate(rows, axis=0)
                return c

            lax.fori_loop(0, half // strip, some, 0)
            remote(part.at[h], gather.at[h], send, ex_recv.at[h], partner).start()

    gradient(rs1, ar_recv1, rrow, -1.0, part1, gather1, ex_send.at[0], ex_recv1, lambda: None)
    for h in range(2):
        drain(gather1.at[h], ex_recv1.at[h])
        rows = slice(h * half, (h + 1) * half)
        g = w_v[rows] * (part1[h] + gather1[h])
        grow[rows] = g
        urow[rows] = w_v[rows] * g
        if h == 0:
            forward(0, 0, False)
            forward(1, 0, False)
    g = grow[...]
    broadcast(jnp.sum(g * g, axis=0, keepdims=True), gout, gmsg, 0)

    def image(b, c):
        @pl.when(b >= 2)
        def _():
            forward(b, 0, False)

        forward(b, 1, True)
        send_rows(block_rows(b), out2, rs2, ar_recv2, b, 1)
        return c

    lax.fori_loop(0, nz, image, 0)

    def send_delta():
        q = qrow[...]
        dout[...] = jnp.sum(jnp.sum(q * q, axis=0), axis=0, keepdims=True)
        remote(dout, din, sc_send.at[1], sc_recv.at[1], partner).start()

    gradient(rs2, ar_recv2, qrow, 1.0, part2, gather2, ex_send.at[1], ex_recv2, send_delta)

    def total(msgs, which):
        drain(msgs.at[pl.ds(0, chips - 1)], sc_recv.at[which])
        return jnp.sum(jnp.sum(msgs[...], axis=0), axis=1, keepdims=True)

    gamma = total(gmsg, 0)
    drain(din, sc_recv.at[1])
    alpha = gamma / jnp.sum(dout[...] + din[...], axis=1, keepdims=True)

    own = pl.ds(pl.multiple_of(core * half, half), half)
    model_ref[...] = m_all[core] + alpha * grow[own]
    new = rrow[z] - alpha * qrow[z]
    mine = jnp.zeros((1, LANES), F32)
    for q in range(n_cell):
        tile, at = q // per_tile, q % per_tile
        value = new[tile:tile + 1]
        if at:
            value = pltpu.roll(value, LANES - at * piece, 1)
        mine = jnp.where(my_cell == q, value, mine)
    res_ref[...] = mine[:, :piece]

    square = jnp.zeros((half, LANES), F32)
    for h in range(2):
        drain(gather2.at[h], ex_recv2.at[h])
        rows = slice(h * half, (h + 1) * half)
        g = grow[rows] - alpha * (w_v[rows] * (part2[h] + gather2[h]))
        urow[rows] = g
        square += g * g
    broadcast(jnp.sum(square, axis=0, keepdims=True), gnout, gnmsg, 2)
    beta = total(gnmsg, 2) / gamma
    search_ref[...] = urow[own] + beta * grow[own]

    drain(st_all.at[pl.ds(0, nz - 1)], st_send)
    drain(m_all.at[0], m_sem.at[0])
    drain(rs1.at[:, pl.ds(0, chips - 1)], ar_send.at[0])
    drain(rs2.at[:, pl.ds(0, chips - 1)], ar_send.at[1])
    drain(part1, ex_send.at[0])
    drain(part2, ex_send.at[1])
    drain(gmsg.at[pl.ds(0, chips - 1)], sc_send.at[0])
    drain(din, sc_send.at[1])
    drain(gnmsg.at[pl.ds(0, chips - 1)], sc_send.at[2])


def per_device(station_xyz, cell_xyz, cell_weight, data, model_start):
    n_sta, n_cell = lax.axis_size("sta"), lax.axis_size("cell")
    n = n_sta * n_cell
    width = station_xyz.shape[1]
    cells = model_start.shape[0]
    piece = data.shape[0]
    scale = 1.0 / math.sqrt(width * n_sta * cells * n)
    sizes = (n_sta, n_cell, cells, width, piece, scale)
    nz = n_sta // 2
    chips = nz * n_cell
    tiles, half = 2 * cells // LANES, cells // LANES
    groups, high = width // 8, width // LANES
    hbm = pl.BlockSpec(memory_space=pltpu.HBM)
    vmem = pl.BlockSpec(memory_space=pltpu.VMEM)
    spread = pltpu.VMEM((nz * groups, 8, LANES), F32)
    narrow = pltpu.VMEM((groups, 8, LANES), F32)
    lines = pltpu.VMEM((nz, high, LANES), F32)
    whole = pltpu.VMEM((nz, chips, high, LANES), F32)
    halves = pltpu.VMEM((2, half, LANES), F32)
    packed = pltpu.VMEM((tiles, LANES), F32)
    message = pltpu.VMEM((chips, 1, LANES), F32)
    row = pltpu.VMEM((1, LANES), F32)
    dma = pltpu.SemaphoreType.DMA
    model_next, residual, search = pl.pallas_call(
        functools.partial(kernel, sizes),
        out_shape=(jax.ShapeDtypeStruct((half, LANES), F32), jax.ShapeDtypeStruct((1, piece), F32),
                   jax.ShapeDtypeStruct((half, LANES), F32)),
        in_specs=[hbm, hbm, hbm, hbm, vmem],
        out_specs=(vmem, vmem, vmem),
        scratch_shapes=[
            pltpu.VMEM((nz * groups, 8, 2 * cells), F32),
            pltpu.VMEM((FEATURES, 2 * cells), BF16),
            pltpu.VMEM((width, FEATURES), BF16),
            pltpu.VMEM((3, 2 * cells), F32),
            packed, halves,
            pltpu.VMEM((nz, 3, width), F32),
            narrow, packed, spread,
            pltpu.VMEM((tiles, 8, LANES), F32),
            narrow, lines, lines, packed,
            lines, lines, whole, whole,
            halves, halves, halves, halves,
            message, message, row, row, row, row,
            pltpu.VMEM((high, LANES), F32),
            dma((4,)), dma, dma((nz,)), dma((2,)), dma((2,)), dma((nz,)), dma((nz,)),
            dma((2,)), dma((2,)), dma((2,)), dma((3,)), dma((3,)),
            pltpu.VMEM((groups, 8, 512), F32), pltpu.VMEM((groups, 8, 512), F32),
        ],
        compiler_params=pltpu.CompilerParams(
            collective_id=0, has_side_effects=True, vmem_limit_bytes=60 * 1024 * 1024),
    )(station_xyz, cell_xyz, cell_weight.reshape(-1, LANES), model_start.reshape(-1, LANES),
      data.reshape(1, piece))
    return (model_next.reshape(cells), residual.reshape(piece), search.reshape(cells))


def solution(mesh):
    placed = (P(None, "sta"), P(None, "cell"), P("cell"), P(("sta", "cell")), P(("cell", "sta")))
    return jax.shard_map(
        per_device,
        mesh=mesh,
        in_specs=placed,
        out_specs=(P(("cell", "sta")), P(("sta", "cell")), P(("cell", "sta"))),
        check_vma=False,
    )
```

time: 67.2 us -> 50.7 us (0.75)
  Pallas kernels: 58.9 us -> 47.4 us
  local copies, waits for them, and re-layouts: 7.33 us -> 2.46 us
    pallas_call x1, Pallas kernels: 58.9 us -> 47.4 us  [per_device(): pl.pallas_call(functools.partial(kernel, sizes), out_shape=(jax.ShapeDtyp...]
    dynamic_slice x2 -> x0, local copies, waits for them, and re-layouts: 1.35 us -> none  [the longest x1 1.34 us: per_device(): lax.dynamic_slice_in_dim(cell_weight, at, cells, 0).reshape(1, cells)]
    pad x2 -> x0, local copies, waits for them, and re-layouts: 1.26 us -> none  [the longest x1 0.66 us: per_device(): jnp.pad(lax.dynamic_slice_in_dim(cell_xyz, at, cells, 1), ((0, 5), (0, 0)))]
    unnamed x12 -> x7, local copies, waits for them, and re-layouts: 3.7 us -> 2.46 us
where the time goes in v1:
time: 50.7 us; the launch traced here: 50.5 us
  Pallas kernels  47.4 us (93%)
  local copies, waits for them, and re-layouts  2.46 us (5%)
  between operations  0.66 us (1%)
    pallas_call x1, Pallas kernels, per_device(): pl.pallas_call(functools.partial(kernel, sizes), out_shape=(jax.ShapeDtyp...  47.4 us
    unnamed x7, local copies, waits for them, and re-layouts  2.46 us

profile of v1, /device:TPU:0, one launch (start us, length us, event | category | flops | bytes accessed | tf_op | source)
XLA Modules:
  0.0 50.5 jit_solution(15058471782049830894)
XLA Ops:
  0.6 47.4 %shard_map.76 = (f32[32,128]{1,0:T(8,128)}, f32[1,64]{1,0:T(1,128)}, f32[32,128]{1,0:T(8,128)}) custom-call(f32[3,256]{1,0:T(4,128)} %st_hbm.1, f32[3,32768]{1,0:T(4,128)} %cell_hbm.1, f32[256,128]{1,0:T(8,128)} %bitcast.6, f32[32,128]{1,0:T(8,128)} %bitcast.7, f32[1,64]{1,0:T(1,128)} %bitcast.10), custom_call_target="tpu_custom_call" | custom-call | tf_op jit(solution)/shard_map/pallas_call | solution.py:418
  48.1 0.0 copy-start.1
  48.1 0.0 copy-start
  48.1 1.3 %copy.11 = f32[4096]{0:T(1024)} copy(f32[4096]{0:T(1024)} %bitcast.9) | data formatting | bytes 32768
  49.4 0.0 copy-done.1
  49.4 0.5 %copy.12 = f32[64]{0:T(128)} copy(f32[64]{0:T(128)S(1)} %bitcast.11) | data formatting | bytes 512
  49.9 0.0 copy-done
  49.9 0.6 %copy.13 = f32[4096]{0:T(1024)} copy(f32[4096]{0:T(1024)S(1)} %bitcast.8) | data formatting | bytes 32768
Async XLA Ops:
  48.1 1.4 %copy-start.1 = (f32[1,64]{1,0:T(1,128)S(1)}, f32[1,64]{1,0:T(1,128)}, u32[]{:S(2)}) copy-start(f32[1,64]{1,0:T(1,128)} %get-tuple-element.7) | copy-start | bytes 772
  48.1 1.9 %copy-start = (f32[32,128]{1,0:T(8,128)S(1)}, f32[32,128]{1,0:T(8,128)}, u32[]{:S(2)}) copy-start(f32[32,128]{1,0:T(8,128)} %get-tuple-element.8) | copy-start | bytes 49156

commit v2 on v1

--- a/solution.py
+++ b/solution.py
@@ -71,11 +71,11 @@
                             ones, pair(a1, a2) + soft, pair(b1, b2) + rest, zero], axis=0)
 
 
-def kernel(sizes, st_hbm, cell_hbm, w_hbm, m_hbm, data_ref, model_ref, res_ref, search_ref,
+def kernel(sizes, st_hbm, cell_hbm, w_hbm, m_hbm, data_hbm, model_ref, res_ref, search_ref,
            kmat, rhs, lhs, cell_v, w_v, m_all, st_all, szb, urow, acc, gacc, rb, rrow, qrow, grow,
            out1, out2, rs1, rs2, part1, part2, gather1, gather2, gmsg, gnmsg, gout, gnout, dout, din, drow,
            in_sem, st_send, st_recv, m_sem, ar_send, ar_recv1, ar_recv2, ex_send, ex_recv1, ex_recv2,
-           sc_send, sc_recv, r2a, r2b):
+           sc_send, sc_recv, data_v):
     n_sta, n_cell, cells, width, piece, scale = sizes
     nz = n_sta // 2
     chips = nz * n_cell
@@ -122,6 +122,8 @@
     load_stations.start()
     load_weights.start()
     load_model.start()
+    load_data = pltpu.make_async_copy(data_hbm, data_v, in_sem.at[4])
+    load_data.start()
 
     barrier = pltpu.get_barrier_semaphore()
 
@@ -145,40 +147,29 @@
             zz = jnp.transpose(jnp.broadcast_to(x[2:3, cols], (LANES, LANES)))
             szb[i * 16:(i + 1) * 16] = zz.reshape(16, 8, LANES)
 
-    block = 512
-    per_block = block // LANES
-
-    def distances(n, r2):
-        cols = pl.ds(pl.multiple_of(n * block, block), block)
-        r2[...] = jnp.dot(lhs[...], rhs[:, cols], preferred_element_type=F32).reshape(groups, 8, block)
-
-    def values(b, n, r2):
-        at = n * block
-        czs = []
-        cols = []
-        for t in range(per_block):
-            cols.append(pl.ds(pl.multiple_of(at + t * LANES, LANES), LANES))
-            czs.append(jnp.broadcast_to(cell_v[2:3, cols[t]], (8, LANES)))
-        for g in range(groups):
-            sz = szb[g]
-            for t in range(per_block):
-                inv = lax.rsqrt(r2[g, :, t * LANES:(t + 1) * LANES])
-                kmat[b * groups + g, :, cols[t]] = ((sz - czs[t]) * inv) * (inv * inv)
-
-    def build(b):
-        count = 2 * cells // block
-        distances(0, r2a)
-
-        def one(i, c):
-            distances(i * 2 + 1, r2b)
-            values(b, i * 2, r2a)
-            distances(lax.rem(i * 2 + 2, count), r2a)
-            values(b, i * 2 + 1, r2b)
+    block = min(2048, 2 * cells)
+
+    def build(b, n):
+        at = pl.multiple_of(n * block, block)
+        r2 = jnp.dot(lhs[...], rhs[:, pl.ds(at, block)], preferred_element_type=F32)
+        r2 = r2.reshape(groups, 8, block)
+        cz = cell_v[2:3, pl.ds(at, block)]
+        out = []
+        for t in range(block // LANES):
+            cols = slice(t * LANES, (t + 1) * LANES)
+            inv = lax.rsqrt(r2[:, :, cols])
+            dz = szb[...] - jnp.broadcast_to(cz[:, cols], (8, LANES))[None]
+            out.append((dz * inv) * (inv * inv))
+        kmat[pl.ds(b * groups, groups), :, pl.ds(at, block)] = jnp.concatenate(out, axis=2)
+
+    def build_from(b, first):
+        def one(n, c):
+            build(b, n)
             return c
 
-        lax.fori_loop(0, count // 2, one, 0)
-
-    step = 4
+        lax.fori_loop(first, 2 * cells // block, one, 0)
+
+    step = 8
 
     def forward(b, h, add):
         us = [jnp.broadcast_to(urow[pl.ds(h * half + t, 1), :], (8, LANES)) for t in range(half)]
@@ -227,8 +218,7 @@
 
     load_stations.wait()
     prepare(z)
-    build(z)
-
+    build(z, 0)
     pl.semaphore_wait(barrier, chips)
 
     def send_stations(k, c):
@@ -239,13 +229,15 @@
     lax.fori_loop(1, nz, send_stations, 0)
     load_model.wait()
     remote(m_all.at[core], m_all.at[core], m_sem.at[0], m_sem.at[1], partner).start()
+    build_from(z, 1)
     load_weights.wait()
     ws = w_v[...] * scale
     w_v[...] = ws
     drain(m_all.at[0], m_sem.at[1])
     urow[...] = ws * m_all[...].reshape(tiles, LANES)
 
-    data = data_ref[...]
+    load_data.wait()
+    data = data_v[...]
     drow[...] = jnp.zeros((high, LANES), F32)
     lane = lax.broadcasted_iota(jnp.int32, (1, LANES), 1)
     wide = jnp.where(lane < piece, jnp.concatenate([data] * per_tile, axis=1), 0.0)
@@ -262,7 +254,7 @@
         b = order(k)
         drain(st_all.at[b], st_recv.at[b])
         prepare(b)
-        build(b)
+        build_from(b, 0)
         forward(b, 0, False)
         forward(b, 1, True)
         send_rows(block_rows(b), out1, rs1, ar_recv1, b)
@@ -278,18 +270,12 @@
             x = jnp.transpose(jnp.broadcast_to(row[i:i + 1], (LANES, LANES)))
             rb[i * 16:(i + 1) * 16] = x.reshape(16, 8, LANES)
 
-    strip = 8
+    strip = 16
 
     def backward(b, at):
-        rs_ = [rb[g] for g in range(groups)]
-        cols = [pl.ds(pl.multiple_of((at + t) * LANES, LANES), LANES) for t in range(strip)]
-        out = []
-        for t in range(strip):
-            total = gacc[at + t]
-            for g in range(groups):
-                total = total + kmat[b * groups + g, :, cols[t]] * rs_[g]
-            out.append(total)
-        return out
+        x = kmat[pl.ds(b * groups, groups), :, pl.ds(pl.multiple_of(at * LANES, LANES), strip * LANES)]
+        return [gacc[at + t] + jnp.sum(x[:, :, t * LANES:(t + 1) * LANES] * rb[...], axis=0)
+                for t in range(strip)]
 
     def gradient(rs, recv, store, sign, part, gather, send, ex_recv, complete):
         gacc[...] = jnp.zeros((tiles, 8, LANES), F32)
@@ -327,13 +313,15 @@
         grow[rows] = g
         urow[rows] = w_v[rows] * g
         if h == 0:
-            forward(0, 0, False)
-            forward(1, 0, False)
+            forward(settled(0), 0, False)
+            forward(settled(1), 0, False)
     g = grow[...]
     broadcast(jnp.sum(g * g, axis=0, keepdims=True), gout, gmsg, 0)
 
-    def image(b, c):
-        @pl.when(b >= 2)
+    def image(j, c):
+        b = settled(j)
+
+        @pl.when(j >= 2)
         def _():
             forward(b, 0, False)
 
@@ -419,7 +407,7 @@
         functools.partial(kernel, sizes),
         out_shape=(jax.ShapeDtypeStruct((half, LANES), F32), jax.ShapeDtypeStruct((1, piece), F32),
                    jax.ShapeDtypeStruct((half, LANES), F32)),
-        in_specs=[hbm, hbm, hbm, hbm, vmem],
+        in_specs=[hbm] * 5,
         out_specs=(vmem, vmem, vmem),
         scratch_shapes=[
             pltpu.VMEM((nz * groups, 8, 2 * cells), F32),
@@ -435,9 +423,9 @@
             halves, halves, halves, halves,
             message, message, row, row, row, row,
             pltpu.VMEM((high, LANES), F32),
-            dma((4,)), dma, dma((nz,)), dma((2,)), dma((2,)), dma((nz,)), dma((nz,)),
+            dma((5,)), dma, dma((nz,)), dma((2,)), dma((2,)), dma((nz,)), dma((nz,)),
             dma((2,)), dma((2,)), dma((2,)), dma((3,)), dma((3,)),
-            pltpu.VMEM((groups, 8, 512), F32), pltpu.VMEM((groups, 8, 512), F32),
+            pltpu.VMEM((1, piece), F32),
         ],
         compiler_params=pltpu.CompilerParams(
             collective_id=0, has_side_effects=True, vmem_limit_bytes=60 * 1024 * 1024),

time: 50.7 us -> 41.6 us (0.82)
  Pallas kernels: 47.4 us -> 38.3 us
    pallas_call x1, Pallas kernels: 47.4 us -> 38.3 us  [per_device(): pl.pallas_call(functools.partial(kernel, sizes), out_shape=(jax.ShapeDtyp...]
where the time goes in v2:
time: 41.6 us; the launch traced here: 41.5 us
  Pallas kernels  38.3 us (92%)
  local copies, waits for them, and re-layouts  2.46 us (6%)
  between operations  0.66 us (2%)
    pallas_call x1, Pallas kernels, per_device(): pl.pallas_call(functools.partial(kernel, sizes), out_shape=(jax.ShapeDtyp...  38.3 us
    unnamed x7, local copies, waits for them, and re-layouts  2.46 us

profile of v2, /device:TPU:0, one launch (start us, length us, event | category | flops | bytes accessed | tf_op | source)
XLA Modules:
  0.0 41.5 jit_solution(2797315028108932239)
XLA Ops:
  0.6 38.3 %shard_map.76 = (f32[32,128]{1,0:T(8,128)}, f32[1,64]{1,0:T(1,128)}, f32[32,128]{1,0:T(8,128)}) custom-call(f32[3,256]{1,0:T(4,128)} %st_hbm.1, f32[3,32768]{1,0:T(4,128)} %cell_hbm.1, f32[256,128]{1,0:T(8,128)} %bitcast.6, f32[32,128]{1,0:T(8,128)} %bitcast.7, f32[1,64]{1,0:T(1,128)} %bitcast.10), custom_call_target="tpu_custom_call" | custom-call | tf_op jit(solution)/shard_map/pallas_call | solution.py:406
  39.0 0.0 copy-start.1
  39.0 0.0 copy-start
  39.0 1.3 %copy.11 = f32[4096]{0:T(1024)} copy(f32[4096]{0:T(1024)} %bitcast.9) | data formatting | bytes 32768
  40.3 0.0 copy-done.1
  40.3 0.5 %copy.12 = f32[64]{0:T(128)} copy(f32[64]{0:T(128)S(1)} %bitcast.11) | data formatting | bytes 512
  40.8 0.0 copy-done
  40.9 0.6 %copy.13 = f32[4096]{0:T(1024)} copy(f32[4096]{0:T(1024)S(1)} %bitcast.8) | data formatting | bytes 32768
Async XLA Ops:
  39.0 1.4 %copy-start.1 = (f32[1,64]{1,0:T(1,128)S(1)}, f32[1,64]{1,0:T(1,128)}, u32[]{:S(2)}) copy-start(f32[1,64]{1,0:T(1,128)} %get-tuple-element.7) | copy-start | bytes 772
  39.0 1.9 %copy-start = (f32[32,128]{1,0:T(8,128)S(1)}, f32[32,128]{1,0:T(8,128)}, u32[]{:S(2)}) copy-start(f32[32,128]{1,0:T(8,128)} %get-tuple-element.8) | copy-start | bytes 49156

commit v3 on v2

--- a/solution.py
+++ b/solution.py
@@ -102,7 +102,7 @@
 
             lax.fori_loop(1, chips, one, 0)
         else:
-            for k in range(1, chips):
+            for k in range(chips - 1, 0, -1):
                 act((my_sta ^ (k // n_cell * 2), my_cell ^ (k % n_cell)))
 
     def remote(src, dst, send, recv, device):
@@ -111,6 +111,11 @@
 
     def drain(ref, sem):
         pltpu.make_async_copy(ref, ref, sem).wait()
+
+    barrier = pltpu.get_barrier_semaphore()
+
+    every_peer(lambda device: pl.semaphore_signal(barrier, inc=1, device_id=device, device_id_type=MESH))
+    pl.semaphore_signal(barrier, inc=1, device_id=partner, device_id_type=MESH)
 
     first_cell = pl.multiple_of(z * 2 * cells, 2 * cells)
     first_row = pl.multiple_of(z * tiles, tiles)
@@ -125,11 +130,6 @@
     load_data = pltpu.make_async_copy(data_hbm, data_v, in_sem.at[4])
     load_data.start()
 
-    barrier = pltpu.get_barrier_semaphore()
-
-    every_peer(lambda device: pl.semaphore_signal(barrier, inc=1, device_id=device, device_id_type=MESH))
-    pl.semaphore_signal(barrier, inc=1, device_id=partner, device_id_type=MESH)
-
     def features(n, c):
         cols = pl.ds(pl.multiple_of(n * 512, 512), 512)
         rhs[:, cols] = cell_features(eight_rows(cell_v[:, cols]))
@@ -248,19 +248,20 @@
 
     forward(z, 0, False)
     forward(z, 1, True)
-    send_rows(block_rows(z) - drow[...], out1, rs1, ar_recv1, z)
 
     def rest(k, c):
         b = order(k)
         drain(st_all.at[b], st_recv.at[b])
+        rows = block_rows(order(k - 1)) - jnp.where(k == 1, drow[...], 0.0)
         prepare(b)
+        send_rows(rows, out1, rs1, ar_recv1, order(k - 1))
         build_from(b, 0)
         forward(b, 0, False)
         forward(b, 1, True)
-        send_rows(block_rows(b), out1, rs1, ar_recv1, b)
         return c
 
     lax.fori_loop(1, nz, rest, 0)
+    send_rows(block_rows(order(nz - 1)), out1, rs1, ar_recv1, order(nz - 1))
 
     def arrive(b, rs, recv, store, sign):
         drain(rs.at[b, pl.ds(0, chips - 1)], recv.at[b])
@@ -428,9 +429,21 @@
             pltpu.VMEM((1, piece), F32),
         ],
         compiler_params=pltpu.CompilerParams(
-            collective_id=0, has_side_effects=True, vmem_limit_bytes=60 * 1024 * 1024),
-    )(station_xyz, cell_xyz, cell_weight.reshape(-1, LANES), model_start.reshape(-1, LANES),
-      data.reshape(1, piece))
+            collective_id=0, has_side_effects=True, vmem_limit_bytes=48 * 1024 * 1024),
+    )(*[pltpu.with_memory_space_constraint(x, pltpu.HBM) for x in (station_xyz, cell_xyz, cell_weight.reshape(-1, LANES), model_start.reshape(-1, LANES),
+      data.reshape(1, piece))])
+    def hand(a, b, c, x, y, z):
+        x[...] = a[...]
+        y[...] = b[...]
+        z[...] = c[...]
+
+    model_next, residual, search = pl.pallas_call(
+        hand,
+        out_shape=(jax.ShapeDtypeStruct((half, LANES), F32), jax.ShapeDtypeStruct((1, piece), F32),
+                   jax.ShapeDtypeStruct((half, LANES), F32)),
+        in_specs=[vmem] * 3, out_specs=(vmem, vmem, vmem),
+        compiler_params=pltpu.CompilerParams(vmem_limit_bytes=1024 * 1024),
+    )(model_next, residual, search)
     return (model_next.reshape(cells), residual.reshape(piece), search.reshape(cells))
 
 

time: 41.6 us -> 38.6 us (0.928)
  local copies, waits for them, and re-layouts: 2.46 us -> 0 us
  Pallas kernels: 38.3 us -> 37.8 us
    unnamed x7 -> x0, local copies, waits for them, and re-layouts: 2.46 us -> none
    pallas_call x1, Pallas kernels: 38.3 us -> 37.2 us  [per_device(): pl.pallas_call(functools.partial(kernel, sizes), out_shape=(jax.ShapeDtyp...]
    pallas_call x0 -> x1, Pallas kernels: none -> 0.62 us  [per_device(): pl.pallas_call(hand, out_shape=(jax.ShapeDtypeStruct((half, LANES), F32),...]
where the time goes in v3:
time: 38.6 us; the launch traced here: 38.4 us
  Pallas kernels  37.8 us (98%)
  between operations  0.64 us (2%)
    pallas_call x1, Pallas kernels, per_device(): pl.pallas_call(functools.partial(kernel, sizes), out_shape=(jax.ShapeDtyp...  37.2 us

profile of v3, /device:TPU:0, one launch (start us, length us, event | category | flops | bytes accessed | tf_op | source)
XLA Modules:
  0.0 38.4 jit_solution(18133479972157358573)
XLA Ops:
  0.6 37.2 %shard_map.76 = (f32[32,128]{1,0:T(8,128)S(1)}, f32[1,64]{1,0:T(1,128)S(1)}, f32[32,128]{1,0:T(8,128)S(1)}) custom-call(f32[3,256]{1,0:T(4,128)} %st_hbm.1, f32[3,32768]{1,0:T(4,128)} %cell_hbm.1, f32[256,128]{1,0:T(8,128)} %bitcast.6, f32[32,128]{1,0:T(8,128)} %bitcast.7, f32[1,64]{1,0:T(1,128)} %bitcast.8), custom_call_target="tpu_custom_call" | custom-call | tf_op jit(solution)/shard_map/pallas_call | solution.py:407
  37.8 0.6 %shard_map.77 = (f32[32,128]{1,0:T(8,128)}, f32[1,64]{1,0:T(1,128)}, f32[32,128]{1,0:T(8,128)}) custom-call(f32[32,128]{1,0:T(8,128)S(1)} %get-tuple-element.9.a, f32[1,64]{1,0:T(1,128)S(1)} %get-tuple-element.10.b, f32[32,128]{1,0:T(8,128)S(1)} %get-tuple-element.11.c), custom_call_target="tpu_custom_call" | custom-call | tf_op jit(solution)/shard_map/pallas_call | solution.py:440

commit v4 on v3

--- a/solution.py
+++ b/solution.py
@@ -209,27 +209,39 @@
         every_peer(lambda device: remote(out, msgs.at[chip], sc_send.at[which], sc_recv.at[which],
                                          device).start())
 
+    low = z < nz // 2
+
     def order(k):
-        return jnp.where(k <= z, z - k, k)
+        if nz & (nz - 1):
+            return lax.rem(z + k, nz)
+        return z ^ jnp.where(low & (k > 0), jnp.where(k == nz - 1, 1, k + 1), k)
+
+    def fixed(j):
+        return nz - 1 - j
 
     def settled(j):
-        mid = nz // 2
-        return jnp.where(lax.rem(j, 2) == 0, mid - 1 - lax.div(j, 2), mid + lax.div(j, 2))
+        return jnp.where(j < nz - 2, nz - 1 - j, jnp.where(low, nz - 1 - j, j - nz + 2))
 
     load_stations.wait()
     prepare(z)
+
+    def enter():
+        pl.semaphore_wait(barrier, chips)
+
+        def send_stations(k, c):
+            other = lax.rem(z + k, nz)
+            remote(st_all.at[z], st_all.at[z], st_send, st_recv.at[z], (other * 2 + core, my_cell)).start()
+            return c
+
+        lax.fori_loop(1, nz, send_stations, 0)
+        remote(m_all.at[core], m_all.at[core], m_sem.at[0], m_sem.at[1], partner).start()
+
+    load_model.wait()
+    pl.when((z == nz - 1) & (z > 0))(enter)
     build(z, 0)
-    pl.semaphore_wait(barrier, chips)
-
-    def send_stations(k, c):
-        other = lax.rem(z + k, nz)
-        remote(st_all.at[z], st_all.at[z], st_send, st_recv.at[z], (other * 2 + core, my_cell)).start()
-        return c
-
-    lax.fori_loop(1, nz, send_stations, 0)
-    load_model.wait()
-    remote(m_all.at[core], m_all.at[core], m_sem.at[0], m_sem.at[1], partner).start()
+    pl.when((z > 0) & (z < nz - 1))(enter)
     build_from(z, 1)
+    pl.when(z == 0)(enter)
     load_weights.wait()
     ws = w_v[...] * scale
     w_v[...] = ws
@@ -278,11 +290,11 @@
         return [gacc[at + t] + jnp.sum(x[:, :, t * LANES:(t + 1) * LANES] * rb[...], axis=0)
                 for t in range(strip)]
 
-    def gradient(rs, recv, store, sign, part, gather, send, ex_recv, complete):
+    def gradient(turn, rs, recv, store, sign, part, gather, send, ex_recv, complete):
         gacc[...] = jnp.zeros((tiles, 8, LANES), F32)
 
         def early(j, c):
-            b = settled(j)
+            b = turn(j)
             arrive(b, rs, recv, store, sign)
 
             def some(i, c):
@@ -294,7 +306,7 @@
             return c
 
         lax.fori_loop(0, nz - 1, early, 0)
-        b = settled(nz - 1)
+        b = turn(nz - 1)
         arrive(b, rs, recv, store, sign)
         complete()
         for h in range(2):
@@ -306,7 +318,7 @@
             lax.fori_loop(0, half // strip, some, 0)
             remote(part.at[h], gather.at[h], send, ex_recv.at[h], partner).start()
 
-    gradient(rs1, ar_recv1, rrow, -1.0, part1, gather1, ex_send.at[0], ex_recv1, lambda: None)
+    gradient(settled, rs1, ar_recv1, rrow, -1.0, part1, gather1, ex_send.at[0], ex_recv1, lambda: None)
     for h in range(2):
         drain(gather1.at[h], ex_recv1.at[h])
         rows = slice(h * half, (h + 1) * half)
@@ -314,13 +326,13 @@
         grow[rows] = g
         urow[rows] = w_v[rows] * g
         if h == 0:
-            forward(settled(0), 0, False)
-            forward(settled(1), 0, False)
+            forward(fixed(0), 0, False)
+            forward(fixed(1), 0, False)
     g = grow[...]
     broadcast(jnp.sum(g * g, axis=0, keepdims=True), gout, gmsg, 0)
 
     def image(j, c):
-        b = settled(j)
+        b = fixed(j)
 
         @pl.when(j >= 2)
         def _():
@@ -337,7 +349,7 @@
         dout[...] = jnp.sum(jnp.sum(q * q, axis=0), axis=0, keepdims=True)
         remote(dout, din, sc_send.at[1], sc_recv.at[1], partner).start()
 
-    gradient(rs2, ar_recv2, qrow, 1.0, part2, gather2, ex_send.at[1], ex_recv2, send_delta)
+    gradient(fixed, rs2, ar_recv2, qrow, 1.0, part2, gather2, ex_send.at[1], ex_recv2, send_delta)
 
     def total(msgs, which):
         drain(msgs.at[pl.ds(0, chips - 1)], sc_recv.at[which])
@@ -366,7 +378,15 @@
         g = grow[rows] - alpha * (w_v[rows] * (part2[h] + gather2[h]))
         urow[rows] = g
         square += g * g
-    broadcast(jnp.sum(square, axis=0, keepdims=True), gnout, gnmsg, 2)
+    value = jnp.sum(square, axis=0, keepdims=True)
+    gnout[...] = value
+    gnmsg[chip] = value
+
+    def tell(device):
+        for sta in (device[0] ^ 1, device[0]):
+            remote(gnout, gnmsg.at[chip], sc_send.at[2], sc_recv.at[2], (sta, device[1])).start()
+
+    pl.when(core == 1)(lambda: every_peer(tell))
     beta = total(gnmsg, 2) / gamma
     search_ref[...] = urow[own] + beta * grow[own]
 
@@ -378,7 +398,11 @@
     drain(part2, ex_send.at[1])
     drain(gmsg.at[pl.ds(0, chips - 1)], sc_send.at[0])
     drain(din, sc_send.at[1])
-    drain(gnmsg.at[pl.ds(0, chips - 1)], sc_send.at[2])
+
+    @pl.when(core == 1)
+    def _():
+        for _ in range(2):
+            drain(gnmsg.at[pl.ds(0, chips - 1)], sc_send.at[2])
 
 
 def per_device(station_xyz, cell_xyz, cell_weight, data, model_start):

time: 38.6 us -> 37.9 us (0.982)
  Pallas kernels: 37.8 us -> 37.1 us
    pallas_call x1, Pallas kernels: 37.2 us -> 36.5 us  [per_device(): pl.pallas_call(functools.partial(kernel, sizes), out_shape=(jax.ShapeDtyp...]
where the time goes in v4:
time: 37.9 us; the launch traced here: 37.8 us
  Pallas kernels  37.1 us (98%)
  between operations  0.64 us (2%)
    pallas_call x1, Pallas kernels, per_device(): pl.pallas_call(functools.partial(kernel, sizes), out_shape=(jax.ShapeDtyp...  36.5 us

profile of v4, /device:TPU:0, one launch (start us, length us, event | category | flops | bytes accessed | tf_op | source)
XLA Modules:
  0.0 37.8 jit_solution(4514239051161587610)
XLA Ops:
  0.6 36.5 %shard_map.76 = (f32[32,128]{1,0:T(8,128)S(1)}, f32[1,64]{1,0:T(1,128)S(1)}, f32[32,128]{1,0:T(8,128)S(1)}) custom-call(f32[3,256]{1,0:T(4,128)} %st_hbm.1, f32[3,32768]{1,0:T(4,128)} %cell_hbm.1, f32[256,128]{1,0:T(8,128)} %bitcast.6, f32[32,128]{1,0:T(8,128)} %bitcast.7, f32[1,64]{1,0:T(1,128)} %bitcast.8), custom_call_target="tpu_custom_call" | custom-call | tf_op jit(solution)/shard_map/pallas_call | solution.py:431
  37.1 0.6 %shard_map.77 = (f32[32,128]{1,0:T(8,128)}, f32[1,64]{1,0:T(1,128)}, f32[32,128]{1,0:T(8,128)}) custom-call(f32[32,128]{1,0:T(8,128)S(1)} %get-tuple-element.9.a, f32[1,64]{1,0:T(1,128)S(1)} %get-tuple-element.10.b, f32[32,128]{1,0:T(8,128)S(1)} %get-tuple-element.11.c), custom_call_target="tpu_custom_call" | custom-call | tf_op jit(solution)/shard_map/pallas_call | solution.py:464

commit v5 on v4

--- a/solution.py
+++ b/solution.py
@@ -73,7 +73,7 @@
 
 def kernel(sizes, st_hbm, cell_hbm, w_hbm, m_hbm, data_hbm, model_ref, res_ref, search_ref,
            kmat, rhs, lhs, cell_v, w_v, m_all, st_all, szb, urow, acc, gacc, rb, rrow, qrow, grow,
-           out1, out2, rs1, rs2, part1, part2, gather1, gather2, gmsg, gnmsg, gout, gnout, dout, din, drow,
+           out1, out2, rs1, rs2, part1, part2, gather1, gather2, gmsg, gnmsg, gout, gnout, dout, din,
            in_sem, st_send, st_recv, m_sem, ar_send, ar_recv1, ar_recv2, ex_send, ex_recv1, ex_recv2,
            sc_send, sc_recv, data_v):
     n_sta, n_cell, cells, width, piece, scale = sizes
@@ -114,8 +114,11 @@
 
     barrier = pltpu.get_barrier_semaphore()
 
-    every_peer(lambda device: pl.semaphore_signal(barrier, inc=1, device_id=device, device_id_type=MESH))
-    pl.semaphore_signal(barrier, inc=1, device_id=partner, device_id_type=MESH)
+    around = [(lax.rem(z + k, nz) * 2 + core, my_cell) for k in range(1, nz)]
+    around += [(my_sta, lax.rem(my_cell + k, n_cell)) for k in range(1, n_cell)]
+    around.append(partner)
+    for device in around:
+        pl.semaphore_signal(barrier, inc=1, device_id=device, device_id_type=MESH)
 
     first_cell = pl.multiple_of(z * 2 * cells, 2 * cells)
     first_row = pl.multiple_of(z * tiles, tiles)
@@ -123,20 +126,19 @@
     load_stations = pltpu.make_async_copy(st_hbm, st_all.at[z], in_sem.at[1])
     load_weights = pltpu.make_async_copy(w_hbm.at[pl.ds(first_row, tiles)], w_v, in_sem.at[2])
     load_model = pltpu.make_async_copy(m_hbm, m_all.at[core], in_sem.at[3])
+    load_stations.start()
     load_cells.start()
-    load_stations.start()
     load_weights.start()
     load_model.start()
     load_data = pltpu.make_async_copy(data_hbm, data_v, in_sem.at[4])
     load_data.start()
 
+    lot = min(2048, 2 * cells)
+
     def features(n, c):
-        cols = pl.ds(pl.multiple_of(n * 512, 512), 512)
+        cols = pl.ds(pl.multiple_of(n * lot, lot), lot)
         rhs[:, cols] = cell_features(eight_rows(cell_v[:, cols]))
         return c
-
-    load_cells.wait()
-    lax.fori_loop(0, 2 * cells // 512, features, 0)
 
     def prepare(b):
         x = eight_rows(st_all[b])
@@ -195,12 +197,17 @@
             rows.append(jnp.sum(jnp.transpose(x), axis=0, keepdims=True))
         return jnp.concatenate(rows, axis=0)
 
-    def send_rows(rows, out, rs, recv, b, which=0):
+    def keep_rows(rows, out, rs, b):
         out[b] = rows
         rs[b, chip] = rows
 
+    def send_kept(out, rs, recv, b, which):
         every_peer(lambda device: remote(out.at[b], rs.at[b, chip], ar_send.at[which], recv.at[b],
                                          device).start())
+
+    def send_rows(rows, out, rs, recv, b, which=0):
+        keep_rows(rows, out, rs, b)
+        send_kept(out, rs, recv, b, which)
 
     def broadcast(value, out, msgs, which):
         out[...] = value
@@ -212,21 +219,26 @@
     low = z < nz // 2
 
     def order(k):
-        if nz & (nz - 1):
+        if nz < 2 or nz & (nz - 1):
             return lax.rem(z + k, nz)
-        return z ^ jnp.where(low & (k > 0), jnp.where(k == nz - 1, 1, k + 1), k)
+        far = nz // 2
+        return jnp.where(low & (k > 0) & (k <= far), far + k - 1, z ^ jnp.where(low & (k > far), k - far, k))
 
     def fixed(j):
         return nz - 1 - j
 
     def settled(j):
-        return jnp.where(j < nz - 2, nz - 1 - j, jnp.where(low, nz - 1 - j, j - nz + 2))
+        far = nz // 2
+        return jnp.where(j < far, jnp.where(j + far < nz, far + j, j),
+                         jnp.where(low, nz - 1 - j, j - far))
 
     load_stations.wait()
     prepare(z)
+    load_cells.wait()
+    lax.fori_loop(0, 2 * cells // lot, features, 0)
 
     def enter():
-        pl.semaphore_wait(barrier, chips)
+        pl.semaphore_wait(barrier, len(around))
 
         def send_stations(k, c):
             other = lax.rem(z + k, nz)
@@ -248,23 +260,43 @@
     drain(m_all.at[0], m_sem.at[1])
     urow[...] = ws * m_all[...].reshape(tiles, LANES)
 
-    load_data.wait()
-    data = data_v[...]
-    drow[...] = jnp.zeros((high, LANES), F32)
-    lane = lax.broadcasted_iota(jnp.int32, (1, LANES), 1)
-    wide = jnp.where(lane < piece, jnp.concatenate([data] * per_tile, axis=1), 0.0)
-    for q in range(n_cell):
-        tile, at = q // per_tile, q % per_tile
-        value = pltpu.roll(wide, at * piece, 1) if at else wide
-        drow[tile:tile + 1, :] += jnp.where(my_cell == q, value, 0.0)
-
     forward(z, 0, False)
     forward(z, 1, True)
 
+    def stations_of(k):
+        drain(st_all.at[order(k)], st_recv.at[order(k)])
+
+    def own_rows():
+        load_data.wait()
+        lane = lax.broadcasted_iota(jnp.int32, (1, LANES), 1)
+        wide = jnp.where(lane < piece, jnp.concatenate([data_v[...]] * per_tile, axis=1), 0.0)
+        rows = [jnp.zeros((1, LANES), F32)] * high
+        for q in range(n_cell):
+            tile, at = q // per_tile, q % per_tile
+            value = pltpu.roll(wide, at * piece, 1) if at else wide
+            rows[tile] = jnp.where(my_cell == q, value, rows[tile])
+        return block_rows(z) - jnp.concatenate(rows, axis=0)
+
+    if nz > 1:
+        stations_of(1)
+        keep_rows(own_rows(), out1, rs1, z)
+        prepare(order(1))
+        build_from(order(1), 0)
+        forward(order(1), 0, False)
+        forward(order(1), 1, True)
+    else:
+        keep_rows(own_rows(), out1, rs1, z)
+
     def rest(k, c):
         b = order(k)
-        drain(st_all.at[b], st_recv.at[b])
-        rows = block_rows(order(k - 1)) - jnp.where(k == 1, drow[...], 0.0)
+
+        @pl.when(k == 2)
+        def _():
+            for i in range(2, nz):
+                stations_of(i)
+            send_kept(out1, rs1, ar_recv1, z, 0)
+
+        rows = block_rows(order(k - 1))
         prepare(b)
         send_rows(rows, out1, rs1, ar_recv1, order(k - 1))
         build_from(b, 0)
@@ -272,8 +304,11 @@
         forward(b, 1, True)
         return c
 
-    lax.fori_loop(1, nz, rest, 0)
-    send_rows(block_rows(order(nz - 1)), out1, rs1, ar_recv1, order(nz - 1))
+    lax.fori_loop(2, nz, rest, 0)
+    if nz < 3:
+        send_kept(out1, rs1, ar_recv1, z, 0)
+    if nz > 1:
+        send_rows(block_rows(order(nz - 1)), out1, rs1, ar_recv1, order(nz - 1))
 
     def arrive(b, rs, recv, store, sign):
         drain(rs.at[b, pl.ds(0, chips - 1)], recv.at[b])
@@ -447,7 +482,6 @@
             lines, lines, whole, whole,
             halves, halves, halves, halves,
             message, message, row, row, row, row,
-            pltpu.VMEM((high, LANES), F32),
             dma((5,)), dma, dma((nz,)), dma((2,)), dma((2,)), dma((nz,)), dma((nz,)),
             dma((2,)), dma((2,)), dma((2,)), dma((3,)), dma((3,)),
             pltpu.VMEM((1, piece), F32),

time: 37.9 us -> 37.8 us (level)
  no operation moved by 1% of the time
where the time goes in v5:
time: 37.8 us; the launch traced here: 37.6 us
  Pallas kernels  37 us (98%)
  between operations  0.64 us (2%)
    pallas_call x1, Pallas kernels, per_device(): pl.pallas_call(functools.partial(kernel, sizes), out_shape=(jax.ShapeDtyp...  36.3 us

profile of v5, /device:TPU:0, one launch (start us, length us, event | category | flops | bytes accessed | tf_op | source)
XLA Modules:
  0.0 37.6 jit_solution(15929489210745825600)
XLA Ops:
  0.6 36.3 %shard_map.76 = (f32[32,128]{1,0:T(8,128)S(1)}, f32[1,64]{1,0:T(1,128)S(1)}, f32[32,128]{1,0:T(8,128)S(1)}) custom-call(f32[3,256]{1,0:T(4,128)} %st_hbm.1, f32[3,32768]{1,0:T(4,128)} %cell_hbm.1, f32[256,128]{1,0:T(8,128)} %bitcast.6, f32[32,128]{1,0:T(8,128)} %bitcast.7, f32[1,64]{1,0:T(1,128)} %bitcast.8), custom_call_target="tpu_custom_call" | custom-call | tf_op jit(solution)/shard_map/pallas_call | solution.py:466
  37.0 0.6 %shard_map.77 = (f32[32,128]{1,0:T(8,128)}, f32[1,64]{1,0:T(1,128)}, f32[32,128]{1,0:T(8,128)}) custom-call(f32[32,128]{1,0:T(8,128)S(1)} %get-tuple-element.9.a, f32[1,64]{1,0:T(1,128)S(1)} %get-tuple-element.10.b, f32[32,128]{1,0:T(8,128)S(1)} %get-tuple-element.11.c), custom_call_target="tpu_custom_call" | custom-call | tf_op jit(solution)/shard_map/pallas_call | solution.py:498

commit v6 on v5

--- a/solution.py
+++ b/solution.py
@@ -362,14 +362,10 @@
         urow[rows] = w_v[rows] * g
         if h == 0:
             forward(fixed(0), 0, False)
-            forward(fixed(1), 0, False)
-    g = grow[...]
-    broadcast(jnp.sum(g * g, axis=0, keepdims=True), gout, gmsg, 0)
-
     def image(j, c):
         b = fixed(j)
 
-        @pl.when(j >= 2)
+        @pl.when(j >= 1)
         def _():
             forward(b, 0, False)
 
@@ -378,6 +374,8 @@
         return c
 
     lax.fori_loop(0, nz, image, 0)
+    g = grow[...]
+    broadcast(jnp.sum(g * g, axis=0, keepdims=True), gout, gmsg, 0)
 
     def send_delta():
         q = qrow[...]

time: 37.8 us -> 37.4 us (0.989)
  Pallas kernels: 37 us -> 36.6 us
where the time goes in v6:
time: 37.4 us; the launch traced here: 37.3 us
  Pallas kernels  36.6 us (98%)
  between operations  0.64 us (2%)
    pallas_call x1, Pallas kernels, per_device(): pl.pallas_call(functools.partial(kernel, sizes), out_shape=(jax.ShapeDtyp...  36 us

profile of v6, /device:TPU:0, one launch (start us, length us, event | category | flops | bytes accessed | tf_op | source)
XLA Modules:
  0.0 37.3 jit_solution(4469153849038740114)
XLA Ops:
  0.6 36.0 %shard_map.76 = (f32[32,128]{1,0:T(8,128)S(1)}, f32[1,64]{1,0:T(1,128)S(1)}, f32[32,128]{1,0:T(8,128)S(1)}) custom-call(f32[3,256]{1,0:T(4,128)} %st_hbm.1, f32[3,32768]{1,0:T(4,128)} %cell_hbm.1, f32[256,128]{1,0:T(8,128)} %bitcast.6, f32[32,128]{1,0:T(8,128)} %bitcast.7, f32[1,64]{1,0:T(1,128)} %bitcast.8), custom_call_target="tpu_custom_call" | custom-call | tf_op jit(solution)/shard_map/pallas_call | solution.py:464
  36.6 0.6 %shard_map.77 = (f32[32,128]{1,0:T(8,128)}, f32[1,64]{1,0:T(1,128)}, f32[32,128]{1,0:T(8,128)}) custom-call(f32[32,128]{1,0:T(8,128)S(1)} %get-tuple-element.9.a, f32[1,64]{1,0:T(1,128)S(1)} %get-tuple-element.10.b, f32[32,128]{1,0:T(8,128)S(1)} %get-tuple-element.11.c), custom_call_target="tpu_custom_call" | custom-call | tf_op jit(solution)/shard_map/pallas_call | solution.py:496

commit v7 on v6

--- a/solution.py
+++ b/solution.py
@@ -420,9 +420,6 @@
             remote(gnout, gnmsg.at[chip], sc_send.at[2], sc_recv.at[2], (sta, device[1])).start()
 
     pl.when(core == 1)(lambda: every_peer(tell))
-    beta = total(gnmsg, 2) / gamma
-    search_ref[...] = urow[own] + beta * grow[own]
-
     drain(st_all.at[pl.ds(0, nz - 1)], st_send)
     drain(m_all.at[0], m_sem.at[0])
     drain(rs1.at[:, pl.ds(0, chips - 1)], ar_send.at[0])
@@ -431,6 +428,8 @@
     drain(part2, ex_send.at[1])
     drain(gmsg.at[pl.ds(0, chips - 1)], sc_send.at[0])
     drain(din, sc_send.at[1])
+    beta = total(gnmsg, 2) / gamma
+    search_ref[...] = urow[own] + beta * grow[own]
 
     @pl.when(core == 1)
     def _():

time: 37.4 us -> 37.4 us (level)
  no operation moved by 1% of the time
where the time goes in v7:
time: 37.4 us; the launch traced here: 37.2 us
  Pallas kernels  36.6 us (98%)
  between operations  0.64 us (2%)
    pallas_call x1, Pallas kernels, per_device(): pl.pallas_call(functools.partial(kernel, sizes), out_shape=(jax.ShapeDtyp...  36 us

profile of v7, /device:TPU:0, one launch (start us, length us, event | category | flops | bytes accessed | tf_op | source)
XLA Modules:
  0.0 37.2 jit_solution(15897241443166340992)
XLA Ops:
  0.6 36.0 %shard_map.76 = (f32[32,128]{1,0:T(8,128)S(1)}, f32[1,64]{1,0:T(1,128)S(1)}, f32[32,128]{1,0:T(8,128)S(1)}) custom-call(f32[3,256]{1,0:T(4,128)} %st_hbm.1, f32[3,32768]{1,0:T(4,128)} %cell_hbm.1, f32[256,128]{1,0:T(8,128)} %bitcast.6, f32[32,128]{1,0:T(8,128)} %bitcast.7, f32[1,64]{1,0:T(1,128)} %bitcast.8), custom_call_target="tpu_custom_call" | custom-call | tf_op jit(solution)/shard_map/pallas_call | solution.py:463
  36.6 0.6 %shard_map.77 = (f32[32,128]{1,0:T(8,128)}, f32[1,64]{1,0:T(1,128)}, f32[32,128]{1,0:T(8,128)}) custom-call(f32[32,128]{1,0:T(8,128)S(1)} %get-tuple-element.9.a, f32[1,64]{1,0:T(1,128)S(1)} %get-tuple-element.10.b, f32[32,128]{1,0:T(8,128)S(1)} %get-tuple-element.11.c), custom_call_target="tpu_custom_call" | custom-call | tf_op jit(solution)/shard_map/pallas_call | solution.py:495
